TPU v7x, 32 devices: a whole 2x2x4 slice. The times are simulated.
32 devices in a mesh: ta: 4 (over y, x), sa: 8 (over z, core).
Axes of the slice: x: 2, y: 2, z: 4, core: 2. Of those that a mesh axis runs over, the one named last changes fastest.
Arguments:
- eigvecs: float32 [2, 8, 64, 3, 4096], P(None, 'ta', None, None, 'sa'), may hold values from -0.0546875 to 0.0546875
- solutions: float32 [2, 8, 3, 8, 4, 3, 4096], P(None, 'ta', None, None, None, None, 'sa'), may hold values from -15 to 15
- source_times: int32 [3], replicated, may hold values from 0 to 7, as said below
- spin_dilution: int32 [3, 8], replicated, may hold values from 0 to 3
Outputs:
- perambulator: float32 [2, 8, 6144], P(None, 'ta', 'sa')
- norms: float32 [3, 8], replicated
Inputs may be any that keep to these rules, and one draw needn't show every extreme that they name: `source_times`: some source lies at slice 0 and another at slice 8 - 1.
All inputs are finite; a program needn't handle non-finite values.
Results may differ from a plain program's by a relative error of at most 0.000084.
Values sent between devices are 32-bit elements; how exact they have to be, the bound alone decides.
A program may use at most 64 MiB of HBM per device.

v0:
```python
import functools
import math

import jax
import jax.numpy as jnp
from jax import lax
from jax.experimental import pallas as pl
from jax.experimental.pallas import tpu as pltpu
from jax.sharding import PartitionSpec as P

LANES = 128
DIRECT = 64
NT_DIMS = (((1,), (1,)), ((), ()))


def split_two(x):
    high = x.astype(jnp.bfloat16)
    low = (x - high.astype(jnp.float32)).astype(jnp.bfloat16)
    return high, low


def kernel(
    dims,
    eig_hbm, sol_hbm, times_hbm, spin_hbm,
    out_ref, norm_ref,
    eig_buf, sol_buf, left, right_hi, right_lo, tile_buf, flat_buf,
    send_buf, recv_buf, norm_send, norm_recv,
    times_ref, spin_ref, small_sem, own_sem,
    eig_sem, sol_sem, out_sems, in_sems, norm_out_sems, norm_in_sems,
):
    n_ta, n_sa, parts, slices, eigs, colors, sites, srcs, cols, spins, width = dims
    columns = srcs * cols * spins
    rows_own = width // LANES
    blocks = sites // LANES
    my_ta, my_sa = lax.axis_index("ta"), lax.axis_index("sa")

    barrier = pltpu.get_barrier_semaphore()
    one_phase = n_ta * n_sa <= DIRECT
    every = [(a, b) for a in range(n_ta) for b in range(n_sa) if a or b]
    over_sa = [(0, b) for b in range(1, n_sa)]
    over_ta = [(a, 0) for a in range(1, n_ta)]
    first, second = (every, []) if one_phase else (over_sa, over_ta)

    def device(offs):
        return {
            "ta": lax.rem(my_ta + offs[0], n_ta),
            "sa": lax.rem(my_sa + offs[1], n_sa),
        }

    for offs in first + second:
        pl.semaphore_signal(barrier, inc=1, device_id=device(offs))

    small_copies = [
        pltpu.make_async_copy(times_hbm, times_ref, small_sem.at[0]),
        pltpu.make_async_copy(spin_hbm, spin_ref, small_sem.at[1]),
    ]
    for copy in small_copies:
        copy.start()
    sol_copies, eig_copies = {}, {}
    for t in range(slices):
        for c in range(colors):
            for j in range(blocks):
                at = (t * colors + c) * blocks + j
                copy = pltpu.make_async_copy(
                    sol_hbm.at[:, t, :, c, :, pl.ds(j * LANES, LANES)],
                    sol_buf.at[at].reshape(parts, srcs * cols, spins, LANES),
                    sol_sem.at[at],
                )
                copy.start()
                sol_copies[t, c, j] = copy
            copy = pltpu.make_async_copy(
                eig_hbm.at[:, t, c], eig_buf.at[t * colors + c], eig_sem.at[t * colors + c]
            )
            copy.start()
            eig_copies[t, c] = copy

    for copy in small_copies:
        copy.wait()
    lane = lax.broadcasted_iota(jnp.int32, (8, LANES), 1)
    chir = jnp.ones((8, LANES), jnp.float32)
    group = lane // spins
    for s in range(srcs):
        for k in range(cols):
            value = jnp.where(spin_ref[s, k] < 2, 1.0, -1.0)
            chir = jnp.where(group == s * cols + k, value, chir)
    source = lane // (spins * cols)
    signs = []
    for t in range(slices):
        now = my_ta * slices + t
        sign = chir
        for s in range(srcs):
            value = jnp.where(now < times_ref[s], -1.0, 1.0)
            sign = jnp.where(source == s, chir * value, sign)
        signs.append(sign[:1])

    period = math.lcm(columns, LANES)
    rows_in, rows_out = period // columns, period // LANES
    groups = eigs // rows_in
    lane_g = lax.broadcasted_iota(jnp.int32, (groups, LANES), 1)
    copies, owns = {}, []
    rows = parts * rows_own
    sub = math.gcd(rows, 4)

    def make_tiles(t):
        both = lax.dot_general(
            left[t], right_hi[t], NT_DIMS, preferred_element_type=jnp.float32
        )
        cross = lax.dot_general(
            left[t, : parts * eigs, :], right_lo[t], NT_DIMS,
            preferred_element_type=jnp.float32,
        )
        g = both[: parts * eigs] + both[parts * eigs :] + cross
        tiles = (
            g[:eigs, :LANES] + g[eigs:, LANES:],
            g[:eigs, LANES:] - g[eigs:, :LANES],
        )
        for p in range(parts):
            tile_buf[t, p] = tiles[p] * signs[t]
            taken = [tile_buf[t, p, pl.ds(i, groups, stride=rows_in), :] for i in range(rows_in)]
            for o in range(rows_out):
                value, filled = None, 0
                while filled < LANES:
                    i, skip = divmod(o * LANES + filled, columns)
                    size = min(columns - skip, LANES - filled)
                    shift = (filled - skip) % LANES
                    piece = pltpu.roll(taken[i], shift, 1) if shift else taken[i]
                    value = piece if value is None else jnp.where(lane_g < filled, value, piece)
                    filled += size
                flat_buf[t, p, pl.ds(o, groups, stride=rows_out), :] = value
            for d in range(n_sa):
                send_buf[t, pl.ds(d * rows + p * rows_own, rows_own), :] = flat_buf[
                    t, p, pl.ds(d * rows_own, rows_own), :
                ]

    def send_tiles(t):
        sent = send_buf.at[t].reshape(n_sa, rows // sub, sub, LANES)
        landed = recv_buf.at[t].reshape(n_sa, rows // sub, sub, LANES)
        for off in range(1, n_sa):
            peer = lax.rem(my_sa + off, n_sa)
            copy = pltpu.make_async_remote_copy(
                src_ref=sent.at[peer],
                dst_ref=landed.at[off - 1],
                send_sem=out_sems.at[t, off - 1],
                recv_sem=in_sems.at[t, off - 1],
                device_id={"sa": peer},
            )
            copy.start()
            copies[t, off] = copy
        own = pltpu.make_async_copy(sent.at[my_sa], landed.at[n_sa - 1], own_sem.at[t])
        own.start()
        owns.append(own)

    inner = colors * sites
    pad = LANES - columns
    if pad:
        for t in range(slices):
            for p in range(parts):
                spare = pl.ds(p * LANES + columns, pad)
                right_hi[t, spare, :] = jnp.zeros((pad, inner), jnp.bfloat16)
                right_lo[t, spare, :] = jnp.zeros((pad, inner), jnp.bfloat16)
    squares = jnp.zeros((columns, LANES), jnp.float32)
    for t in range(slices):
        for c in range(colors):
            for j in range(blocks):
                sol_copies[t, c, j].wait()
                lanes = pl.ds(c * sites + j * LANES, LANES)
                for p in range(parts):
                    x = sol_buf[(t * colors + c) * blocks + j, p]
                    squares = squares + x * x
                    high, low = split_two(x)
                    right_hi[t, pl.ds(p * LANES, columns), lanes] = high
                    right_lo[t, pl.ds(p * LANES, columns), lanes] = low
            eig_copies[t, c].wait()
            lanes = pl.ds(c * sites, sites)
            for p in range(parts):
                high, low = split_two(eig_buf[t * colors + c, p])
                left[t, pl.ds(p * eigs, eigs), lanes] = high
                left[t, pl.ds((parts + p) * eigs, eigs), lanes] = low
        if t < slices - 1:
            make_tiles(t)

    pl.semaphore_wait(barrier, len(first + second))

    precise = lax.Precision.HIGHEST
    lane_sums = lax.dot_general(
        jnp.ones((8, LANES), jnp.float32), squares, NT_DIMS,
        precision=precise, preferred_element_type=jnp.float32,
    )
    wanted = lax.broadcasted_iota(jnp.int32, (LANES, columns), 0)
    given = lax.broadcasted_iota(jnp.int32, (LANES, columns), 1) // spins
    picks = jnp.where(wanted == given, 1.0, 0.0).astype(jnp.float32)
    own_norm = lax.dot_general(
        lane_sums, picks, NT_DIMS, precision=precise, preferred_element_type=jnp.float32
    )[:1]
    norm_copies = []

    def send_norm(phase, base, peers):
        for at, offs in enumerate(peers):
            copy = pltpu.make_async_remote_copy(
                src_ref=norm_send.at[phase],
                dst_ref=norm_recv.at[base + at],
                send_sem=norm_out_sems.at[base + at],
                recv_sem=norm_in_sems.at[base + at],
                device_id=device(offs),
            )
            copy.start()
            norm_copies.append(copy)

    norm_send[0] = own_norm
    send_norm(0, 0, first)

    for t in range(slices):
        if t == slices - 1:
            make_tiles(t)
        send_tiles(t)

    if second:
        for at, copy in enumerate(norm_copies):
            copy.wait_recv()
            own_norm = own_norm + norm_recv[at]
        norm_send[1] = own_norm
        send_norm(1, len(first), second)

    for t in range(slices):
        owns[t].wait()
        total = recv_buf[t, pl.ds((n_sa - 1) * rows, rows), :]
        for off in range(1, n_sa):
            copies[t, off].wait_recv()
            total = total + recv_buf[t, pl.ds((off - 1) * rows, rows), :]
        for p in range(parts):
            for r in range(rows_own):
                row = p * rows_own + r
                out_ref[p, pl.ds(t, 1), pl.ds(r * LANES, LANES)] = total[row : row + 1]
    landed_from = len(first) if second else 0
    for copy in norm_copies[landed_from:]:
        copy.wait_recv()
    own_norm = own_norm + jnp.sum(norm_recv[landed_from:], axis=0)
    cells = 1.0 * spins * colors * slices * n_ta * sites * n_sa
    own_norm = own_norm / cells
    for s in range(srcs):
        norm_ref[pl.ds(s, 1), :] = own_norm[:, s * cols : (s + 1) * cols]
    for copy in norm_copies:
        copy.wait_send()
    for copy in copies.values():
        copy.wait_send()


def hand_over(tiles_ref, norms_ref, out_ref, norm_ref):
    out_ref[...] = tiles_ref[...]
    norm_ref[...] = norms_ref[...]


def on_device(eigvecs, solutions, source_times, spin_dilution):
    n_ta, n_sa = lax.axis_size("ta"), lax.axis_size("sa")
    parts, slices, eigs, colors, sites = eigvecs.shape
    _, _, srcs, cols, spins, _, _ = solutions.shape
    columns = srcs * cols * spins
    width = eigs * columns // n_sa
    eig_view = jnp.transpose(eigvecs, (0, 1, 3, 2, 4))
    sol_view = jnp.transpose(solutions, (0, 1, 2, 3, 5, 4, 6)).reshape(
        parts, slices, srcs * cols, colors, spins, sites
    )
    dims = (n_ta, n_sa, parts, slices, eigs, colors, sites, srcs, cols, spins, width)
    blocks = sites // LANES
    inner = colors * sites
    rows = parts * (width // LANES)
    norm_peers = n_ta * n_sa - 1 if n_ta * n_sa <= DIRECT else n_ta + n_sa - 2
    f32, bf16 = jnp.float32, jnp.bfloat16
    dma = pltpu.SemaphoreType.DMA
    tiles, norms = pl.pallas_call(
        functools.partial(kernel, dims),
        out_shape=(
            jax.ShapeDtypeStruct((parts, slices, width), f32),
            jax.ShapeDtypeStruct((srcs, cols), f32),
        ),
        in_specs=[
            pl.BlockSpec(memory_space=pltpu.HBM),
            pl.BlockSpec(memory_space=pltpu.HBM),
            pl.BlockSpec(memory_space=pltpu.HBM),
            pl.BlockSpec(memory_space=pltpu.HBM),
        ],
        out_specs=(
            pl.BlockSpec(memory_space=pltpu.VMEM),
            pl.BlockSpec(memory_space=pltpu.VMEM),
        ),
        scratch_shapes=[
            pltpu.VMEM((slices * colors, parts, eigs, sites), f32),
            pltpu.VMEM((slices * colors * blocks, parts, columns, LANES), f32),
            pltpu.VMEM((slices, 2 * parts * eigs, inner), bf16),
            pltpu.VMEM((slices, parts * LANES, inner), bf16),
            pltpu.VMEM((slices, parts * LANES, inner), bf16),
            pltpu.VMEM((slices, parts, eigs, LANES), f32),
            pltpu.VMEM((slices, parts, eigs * columns // LANES, LANES), f32),
            pltpu.VMEM((slices, n_sa * rows, LANES), f32),
            pltpu.VMEM((slices, n_sa * rows, LANES), f32),
            pltpu.VMEM((2, 1, LANES), f32),
            pltpu.VMEM((norm_peers, 1, LANES), f32),
            pltpu.SMEM((srcs,), jnp.int32),
            pltpu.SMEM((srcs, cols), jnp.int32),
            dma((2,)),
            dma((slices,)),
            dma((slices * colors,)),
            dma((slices * colors * blocks,)),
            dma((slices, n_sa - 1)),
            dma((slices, n_sa - 1)),
            dma((norm_peers,)),
            dma((norm_peers,)),
        ],
        compiler_params=pltpu.CompilerParams(collective_id=0, has_side_effects=True),
    )(eig_view, sol_view, source_times, spin_dilution)
    return pl.pallas_call(
        hand_over,
        out_shape=(
            jax.ShapeDtypeStruct(tiles.shape, f32),
            jax.ShapeDtypeStruct(norms.shape, f32),
        ),
    )(tiles, norms)


def solution(mesh):
    return jax.shard_map(
        on_device,
        mesh=mesh,
        in_specs=(
            P(None, "ta", None, None, "sa"),
            P(None, "ta", None, None, None, None, "sa"),
            P(),
            P(),
        ),
        out_specs=(P(None, "ta", "sa"), P()),
        check_vma=False,
    )
```

profile of v0, /device:TPU:0, one launch (start us, length us, event | category | flops | bytes accessed | tf_op | source)
XLA Modules:
  0.0 16.3 jit_solution(6080713991991265448)
XLA Ops:
  0.6 14.4 %shard_map.59 = (f32[2,2,768]{2,1,0:T(2,128)}, f32[3,8]{1,0:T(4,128)}) custom-call(f32[2,2,3,64,512]{4,3,2,1,0:T(8,128)} %bitcast.5, f32[2,2,24,3,4,512]{5,4,3,2,1,0:T(4,128)} %bitcast.4, s32[3]{0:T(128)} %times_hbm.1, s32[3,8]{1,0:T(4,128)} %spin_hbm.1), custom_call_target="tpu_custom_call" | custom-call | tf_op jit(solution)/shard_map/pallas_call | solution.py:270
  15.0 1.3 %shard_map.60 = (f32[2,2,768]{2,1,0:T(2,128)}, f32[3,8]{1,0:T(4,128)}) custom-call(f32[2,2,768]{2,1,0:T(2,128)} %get-tuple-element.4.tiles_ref, f32[3,8]{1,0:T(4,128)} %get-tuple-element.5.norms_ref), custom_call_target="tpu_custom_call" | custom-call | tf_op jit(solution)/shard_map/pallas_call | solution.py:311
where the time goes:
time: 16.5 us; the launch traced here: 16.3 us
  Pallas kernels  15.7 us (95%)
  between operations  0.64 us (4%)
    pallas_call x1, Pallas kernels, on_device(): pl.pallas_call(functools.partial(kernel, dims), out_shape=(jax.ShapeDtype...  14.4 us
    pallas_call x1, Pallas kernels, on_device(): pl.pallas_call(hand_over, out_shape=(jax.ShapeDtypeStruct(tiles.shape, f3...  1.31 us

commit v1 on v0

--- a/solution.py
+++ b/solution.py
@@ -245,9 +245,15 @@
         copy.wait_send()
 
 
-def hand_over(tiles_ref, norms_ref, out_ref, norm_ref):
-    out_ref[...] = tiles_ref[...]
-    norm_ref[...] = norms_ref[...]
+def hand_over(tiles_ref, norms_ref, out_hbm, norm_hbm, sems):
+    copies = [
+        pltpu.make_async_copy(tiles_ref, out_hbm, sems.at[0]),
+        pltpu.make_async_copy(norms_ref, norm_hbm, sems.at[1]),
+    ]
+    for copy in copies:
+        copy.start()
+    for copy in copies:
+        copy.wait()
 
 
 def on_device(eigvecs, solutions, source_times, spin_dilution):
@@ -270,8 +276,8 @@
     tiles, norms = pl.pallas_call(
         functools.partial(kernel, dims),
         out_shape=(
-            jax.ShapeDtypeStruct((parts, slices, width), f32),
-            jax.ShapeDtypeStruct((srcs, cols), f32),
+            pltpu.VMEM((parts, slices, width), f32),
+            pltpu.VMEM((srcs, cols), f32),
         ),
         in_specs=[
             pl.BlockSpec(memory_space=pltpu.HBM),
@@ -306,7 +312,7 @@
             dma((norm_peers,)),
             dma((norm_peers,)),
         ],
-        compiler_params=pltpu.CompilerParams(collective_id=0, has_side_effects=True),
+        compiler_params=pltpu.CompilerParams(collective_id=0, has_side_effects=True, vmem_limit_bytes=66 * 10**6),
     )(eig_view, sol_view, source_times, spin_dilution)
     return pl.pallas_call(
         hand_over,
@@ -314,6 +320,10 @@
             jax.ShapeDtypeStruct(tiles.shape, f32),
             jax.ShapeDtypeStruct(norms.shape, f32),
         ),
+        in_specs=[pl.BlockSpec(memory_space=pltpu.VMEM)] * 2,
+        out_specs=[pl.BlockSpec(memory_space=pltpu.HBM)] * 2,
+        scratch_shapes=[dma((2,))],
+        compiler_params=pltpu.CompilerParams(vmem_limit_bytes=2**20),
     )(tiles, norms)
 
 

time: 16.5 us -> 15.2 us (0.921)
  Pallas kernels: 15.7 us -> 14.4 us
    pallas_call x1, Pallas kernels: 1.31 us -> 0.62 us  [on_device(): pl.pallas_call(hand_over, out_shape=(jax.ShapeDtypeStruct(tiles.shape, f3...]
    pallas_call x1, Pallas kernels: 14.4 us -> 13.8 us  [on_device(): pl.pallas_call(functools.partial(kernel, dims), out_shape=(pltpu.VMEM((pa...]
where the time goes in v1:
time: 15.2 us; the launch traced here: 15 us
  Pallas kernels  14.4 us (95%)
  between operations  0.64 us (4%)
    pallas_call x1, Pallas kernels, on_device(): pl.pallas_call(functools.partial(kernel, dims), out_shape=(pltpu.VMEM((pa...  13.8 us
    pallas_call x1, Pallas kernels, on_device(): pl.pallas_call(hand_over, out_shape=(jax.ShapeDtypeStruct(tiles.shape, f3...  0.62 us

profile of v1, /device:TPU:0, one launch (start us, length us, event | category | flops | bytes accessed | tf_op | source)
XLA Modules:
  0.0 15.0 jit_solution(18107202973794977411)
XLA Ops:
  0.6 13.8 %shard_map.59 = (f32[2,2,768]{2,1,0:T(2,128)S(1)}, f32[3,8]{1,0:T(4,128)S(1)}) custom-call(f32[2,2,3,64,512]{4,3,2,1,0:T(8,128)} %bitcast.5, f32[2,2,24,3,4,512]{5,4,3,2,1,0:T(4,128)} %bitcast.4, s32[3]{0:T(128)} %times_hbm.1, s32[3,8]{1,0:T(4,128)} %spin_hbm.1), custom_call_target="tpu_custom_call" | custom-call | tf_op jit(solution)/shard_map/pallas_call | solution.py:276
  14.4 0.6 %shard_map.60 = (f32[2,2,768]{2,1,0:T(2,128)}, f32[3,8]{1,0:T(4,128)}) custom-call(f32[2,2,768]{2,1,0:T(2,128)S(1)} %get-tuple-element.4.tiles_ref, f32[3,8]{1,0:T(4,128)S(1)} %get-tuple-element.5.norms_ref), custom_call_target="tpu_custom_call" | custom-call | tf_op jit(solution)/shard_map/pallas_call | solution.py:317

commit v2 on v1

v2 whole, which is shorter than its diff:
```python
import functools
import math

import jax
import jax.numpy as jnp
from jax import lax
from jax.experimental import pallas as pl
from jax.experimental.pallas import tpu as pltpu
from jax.sharding import PartitionSpec as P

LANES = 128
SUBLANES = 8
DIRECT = 64
NT_DIMS = (((1,), (1,)), ((), ()))


def split_two(x):
    high = x.astype(jnp.bfloat16)
    low = (x - high.astype(jnp.float32)).astype(jnp.bfloat16)
    return high, low


def others(count, me):
    for k in range(count - 1):
        past = (me <= k).astype(jnp.int32)
        yield k + past, me - 1 + past


def wait_for(ref, sem):
    pltpu.make_async_copy(ref, ref, sem).wait()


def whole_rows(eigs, n_sa):
    return eigs % (SUBLANES * n_sa) == 0


def kernel(
    dims,
    eig_hbm, sol_hbm, times_hbm, spin_hbm,
    out_ref, norm_ref,
    eig_buf, sol_buf, left, right_hi, right_lo, tile_buf, flat_buf,
    send_buf, recv_buf, norm_send, norm_recv,
    times_ref, spin_ref, small_sem,
    eig_sem, sol_sem, out_sems, in_sems, norm_out_sems, norm_in_sems,
):
    n_ta, n_sa, parts, slices, eigs, colors, sites, srcs, cols, spins, width = dims
    columns = srcs * cols * spins
    rows_own = width // LANES
    blocks = sites // LANES
    by_row = whole_rows(eigs, n_sa)
    piece = eigs // n_sa if by_row else rows_own
    rows = parts * piece
    sub = math.gcd(rows, SUBLANES)
    my_ta, my_sa = lax.axis_index("ta"), lax.axis_index("sa")
    barrier = pltpu.get_barrier_semaphore()

    def flat_device(at):
        return {"ta": lax.div(at, n_sa), "sa": lax.rem(at, n_sa)}

    if n_ta * n_sa <= DIRECT:
        groups = [(n_ta * n_sa, my_ta * n_sa + my_sa, flat_device)]
    else:
        groups = [
            (n_sa, my_sa, lambda at: {"sa": at}),
            (n_ta, my_ta, lambda at: {"ta": at}),
        ]
    chunks = [(t, c) for t in range(slices) for c in range(colors)]

    for t, c in chunks:
        for j in range(blocks):
            at = (t * colors + c) * blocks + j
            pltpu.make_async_copy(
                sol_hbm.at[:, t, :, c, :, pl.ds(j * LANES, LANES)],
                sol_buf.at[at].reshape(parts, srcs * cols, spins, LANES),
                sol_sem.at[t * colors + c],
            ).start()
    for count, me, device in groups:
        for peer, _ in others(count, me):
            pl.semaphore_signal(barrier, inc=1, device_id=device(peer))
    for t, c in chunks:
        pltpu.make_async_copy(
            eig_hbm.at[:, t, c], eig_buf.at[t * colors + c], eig_sem.at[t * colors + c]
        ).start()
    small_copies = [
        pltpu.make_async_copy(times_hbm, times_ref, small_sem.at[0]),
        pltpu.make_async_copy(spin_hbm, spin_ref, small_sem.at[1]),
    ]
    for copy in small_copies:
        copy.start()

    inner = colors * sites
    pad = LANES - columns
    if pad:
        for t in range(slices):
            for p in range(parts):
                spare = pl.ds(p * LANES + columns, pad)
                right_hi[t, spare, :] = jnp.zeros((pad, inner), jnp.bfloat16)
                right_lo[t, spare, :] = jnp.zeros((pad, inner), jnp.bfloat16)

    def sol_blocks(t, c):
        for j in range(blocks):
            lanes = pl.ds(c * sites + j * LANES, LANES)
            for p in range(parts):
                yield p, lanes, sol_buf[(t * colors + c) * blocks + j, p]

    def split_sol(t, c):
        for p, lanes, x in sol_blocks(t, c):
            high, low = split_two(x)
            right_hi[t, pl.ds(p * LANES, columns), lanes] = high
            right_lo[t, pl.ds(p * LANES, columns), lanes] = low

    def split_eig(t, c):
        lanes = pl.ds(c * sites, sites)
        for p in range(parts):
            high, low = split_two(eig_buf[t * colors + c, p])
            left[t, pl.ds(p * eigs, eigs), lanes] = high
            left[t, pl.ds((parts + p) * eigs, eigs), lanes] = low

    squares = jnp.zeros((columns, LANES), jnp.float32)
    for t, c in chunks:
        at = t * colors + c
        wait_for(sol_buf.at[pl.ds(at * blocks, blocks)], sol_sem.at[at])
        for _, _, x in sol_blocks(t, c):
            squares = squares + x * x
        if (t, c) != chunks[-1]:
            split_sol(t, c)

    cells = 1.0 * spins * colors * slices * n_ta * sites * n_sa
    sums = jnp.sum(squares, axis=1, keepdims=True) * (1.0 / cells)
    lane = lax.broadcasted_iota(jnp.int32, (columns, LANES), 1)
    group = lax.broadcasted_iota(jnp.int32, (columns, LANES), 0) // spins
    own_norm = jnp.sum(jnp.where(lane == group, sums, 0.0), axis=0, keepdims=True)
    bases = [0, groups[0][0] - 1]

    def send_norm(phase):
        count, me, device = groups[phase]
        for peer, slot in others(count, me):
            pltpu.make_async_remote_copy(
                src_ref=norm_send.at[phase],
                dst_ref=norm_recv.at[bases[phase] + slot],
                send_sem=norm_out_sems.at[phase],
                recv_sem=norm_in_sems.at[phase],
                device_id=device(peer),
            ).start()

    def norm_rows(phase):
        return norm_recv.at[pl.ds(bases[phase], groups[phase][0] - 1)]

    norm_send[0] = own_norm
    pl.semaphore_wait(barrier, sum(count - 1 for count, _, _ in groups))
    send_norm(0)
    split_sol(*chunks[-1])

    def make_signs():
        for copy in small_copies:
            copy.wait()
        lane = lax.broadcasted_iota(jnp.int32, (SUBLANES, LANES), 1)
        chir = jnp.ones((SUBLANES, LANES), jnp.float32)
        for s in range(srcs):
            for k in range(cols):
                value = jnp.where(spin_ref[s, k] < 2, 1.0, -1.0)
                chir = jnp.where(lane // spins == s * cols + k, value, chir)
        signs = []
        for t in range(slices):
            now = my_ta * slices + t
            sign = chir
            for s in range(srcs):
                value = jnp.where(now < times_ref[s], -1.0, 1.0)
                sign = jnp.where(lane // (spins * cols) == s, chir * value, sign)
            signs.append(sign)
        return signs

    def partial(t, c):
        lanes = pl.ds(c * sites, sites)
        both = lax.dot_general(
            left[t, :, lanes], right_hi[t, :, lanes], NT_DIMS,
            preferred_element_type=jnp.float32,
        )
        cross = lax.dot_general(
            left[t, : parts * eigs, lanes], right_lo[t, :, lanes], NT_DIMS,
            preferred_element_type=jnp.float32,
        )
        return both[: parts * eigs] + both[parts * eigs :] + cross

    def flatten(t, p, tile):
        period = math.lcm(columns, LANES)
        rows_in, rows_out = period // columns, period // LANES
        count = eigs // rows_in
        lane = lax.broadcasted_iota(jnp.int32, (count, LANES), 1)
        tile_buf[t, p] = tile
        taken = [tile_buf[t, p, pl.ds(i, count, stride=rows_in), :] for i in range(rows_in)]
        for o in range(rows_out):
            value, filled = None, 0
            while filled < LANES:
                i, skip = divmod(o * LANES + filled, columns)
                size = min(columns - skip, LANES - filled)
                shift = (filled - skip) % LANES
                part = pltpu.roll(taken[i], shift, 1) if shift else taken[i]
                value = part if value is None else jnp.where(lane < filled, value, part)
                filled += size
            flat_buf[t, p, pl.ds(o, count, stride=rows_out), :] = value

    def store_tiles(t, g):
        tiles = (
            g[:eigs, :LANES] + g[eigs:, LANES:],
            g[:eigs, LANES:] - g[eigs:, :LANES],
        )
        for p in range(parts):
            if not by_row:
                flatten(t, p, tiles[p] * signs[t][:1])
            for d in range(n_sa):
                mine = slice(d * piece, (d + 1) * piece)
                send_buf[t, pl.ds(d * rows + p * piece, piece), :] = (
                    tiles[p][mine] if by_row else flat_buf[t, p, mine, :]
                )

    def send_tiles(t):
        sent = send_buf.at[t].reshape(n_sa, rows // sub, sub, LANES)
        landed = recv_buf.at[t].reshape(n_sa - 1, rows // sub, sub, LANES)
        for peer, slot in others(n_sa, my_sa):
            pltpu.make_async_remote_copy(
                src_ref=sent.at[peer],
                dst_ref=landed.at[slot],
                send_sem=out_sems.at[t],
                recv_sem=in_sems.at[t],
                device_id={"sa": peer},
            ).start()

    def step(t, c, g):
        g = partial(t, c) if c == 0 else g + partial(t, c)
        if c == colors - 1:
            store_tiles(t, g)
            send_tiles(t)
        return g

    signs = None if by_row else make_signs()
    g, last = None, None
    for t, c in chunks:
        at = t * colors + c
        wait_for(eig_buf.at[at], eig_sem.at[at])
        split_eig(t, c)
        if last is not None:
            g = step(*last, g)
        last = t, c
    step(*last, g)

    if len(groups) > 1:
        wait_for(norm_rows(0), norm_in_sems.at[0])
        own_norm = own_norm + jnp.sum(norm_rows(0)[...], axis=0)
        norm_send[1] = own_norm
        send_norm(1)

    if by_row:
        signs = make_signs()
    lane_own = lax.broadcasted_iota(jnp.int32, (1, LANES), 1)
    for t in range(slices):
        wait_for(recv_buf.at[t], in_sems.at[t])
        total = send_buf[t, pl.ds(my_sa * rows, rows), :]
        for slot in range(n_sa - 1):
            total = total + recv_buf[t, pl.ds(slot * rows, rows), :]
        for p in range(parts):
            own = total[p * piece : (p + 1) * piece]
            if by_row:
                own = own.reshape(piece // SUBLANES, SUBLANES, LANES) * signs[t]
                own = own.reshape(piece, LANES)
                turned = {}
            for r in range(rows_own):
                if by_row:
                    value, filled = None, 0
                    while filled < LANES:
                        i, skip = divmod(r * LANES + filled, columns)
                        shift = (filled - skip) % LANES
                        if shift not in turned:
                            turned[shift] = pltpu.roll(own, shift, 1) if shift else own
                        part = turned[shift][i : i + 1]
                        value = part if value is None else jnp.where(lane_own < filled, value, part)
                        filled += min(columns - skip, LANES - filled)
                else:
                    value = own[r : r + 1]
                out_ref[p, pl.ds(t, 1), pl.ds(r * LANES, LANES)] = value
        wait_for(recv_buf.at[t], out_sems.at[t])
    for phase in range(len(groups)):
        wait_for(norm_rows(phase), norm_out_sems.at[phase])
    final = len(groups) - 1
    wait_for(norm_rows(final), norm_in_sems.at[final])
    own_norm = own_norm + jnp.sum(norm_rows(final)[...], axis=0)
    for s in range(srcs):
        row = pltpu.roll(own_norm, LANES - s * cols, 1) if s else own_norm
        norm_ref[pl.ds(s, 1), :] = row[:, :cols]


def hand_over(tiles_ref, norms_ref, out_hbm, norm_hbm, sems):
    copies = [
        pltpu.make_async_copy(tiles_ref, out_hbm, sems.at[0]),
        pltpu.make_async_copy(norms_ref, norm_hbm, sems.at[1]),
    ]
    for copy in copies:
        copy.start()
    for copy in copies:
        copy.wait()


def on_device(eigvecs, solutions, source_times, spin_dilution):
    n_ta, n_sa = lax.axis_size("ta"), lax.axis_size("sa")
    parts, slices, eigs, colors, sites = eigvecs.shape
    _, _, srcs, cols, spins, _, _ = solutions.shape
    columns = srcs * cols * spins
    width = eigs * columns // n_sa
    eig_view = jnp.transpose(eigvecs, (0, 1, 3, 2, 4))
    sol_view = jnp.transpose(solutions, (0, 1, 2, 3, 5, 4, 6)).reshape(
        parts, slices, srcs * cols, colors, spins, sites
    )
    dims = (n_ta, n_sa, parts, slices, eigs, colors, sites, srcs, cols, spins, width)
    blocks = sites // LANES
    inner = colors * sites
    rows = parts * (eigs // n_sa if whole_rows(eigs, n_sa) else width // LANES)
    norm_peers = n_ta * n_sa - 1 if n_ta * n_sa <= DIRECT else n_ta + n_sa - 2
    f32, bf16 = jnp.float32, jnp.bfloat16
    dma = pltpu.SemaphoreType.DMA
    tiles, norms = pl.pallas_call(
        functools.partial(kernel, dims),
        out_shape=(
            pltpu.VMEM((parts, slices, width), f32),
            pltpu.VMEM((srcs, cols), f32),
        ),
        in_specs=[
            pl.BlockSpec(memory_space=pltpu.HBM),
            pl.BlockSpec(memory_space=pltpu.HBM),
            pl.BlockSpec(memory_space=pltpu.HBM),
            pl.BlockSpec(memory_space=pltpu.HBM),
        ],
        out_specs=(
            pl.BlockSpec(memory_space=pltpu.VMEM),
            pl.BlockSpec(memory_space=pltpu.VMEM),
        ),
        scratch_shapes=[
            pltpu.VMEM((slices * colors, parts, eigs, sites), f32),
            pltpu.VMEM((slices * colors * blocks, parts, columns, LANES), f32),
            pltpu.VMEM((slices, 2 * parts * eigs, inner), bf16),
            pltpu.VMEM((slices, parts * LANES, inner), bf16),
            pltpu.VMEM((slices, parts * LANES, inner), bf16),
            pltpu.VMEM((slices, parts, eigs, LANES), f32),
            pltpu.VMEM((slices, parts, eigs * columns // LANES, LANES), f32),
            pltpu.VMEM((slices, n_sa * rows, LANES), f32),
            pltpu.VMEM((slices, (n_sa - 1) * rows, LANES), f32),
            pltpu.VMEM((2, 1, LANES), f32),
            pltpu.VMEM((norm_peers, 1, LANES), f32),
            pltpu.SMEM((srcs,), jnp.int32),
            pltpu.SMEM((srcs, cols), jnp.int32),
            dma((2,)),
            dma((slices * colors,)),
            dma((slices * colors,)),
            dma((slices,)),
            dma((slices,)),
            dma((2,)),
            dma((2,)),
        ],
        compiler_params=pltpu.CompilerParams(
            collective_id=0, has_side_effects=True, vmem_limit_bytes=66 * 10**6
        ),
    )(eig_view, sol_view, source_times, spin_dilution)
    return pl.pallas_call(
        hand_over,
        out_shape=(
            jax.ShapeDtypeStruct(tiles.shape, f32),
            jax.ShapeDtypeStruct(norms.shape, f32),
        ),
        in_specs=[pl.BlockSpec(memory_space=pltpu.VMEM)] * 2,
        out_specs=[pl.BlockSpec(memory_space=pltpu.HBM)] * 2,
        scratch_shapes=[dma((2,))],
        compiler_params=pltpu.CompilerParams(vmem_limit_bytes=2**20),
    )(tiles, norms)


def solution(mesh):
    return jax.shard_map(
        on_device,
        mesh=mesh,
        in_specs=(
            P(None, "ta", None, None, "sa"),
            P(None, "ta", None, None, None, None, "sa"),
            P(),
            P(),
        ),
        out_specs=(P(None, "ta", "sa"), P()),
        check_vma=False,
    )
```

time: 15.2 us -> 14.2 us (0.934)
  Pallas kernels: 14.4 us -> 13.4 us
    pallas_call x1, Pallas kernels: 13.8 us -> 12.8 us  [on_device(): pl.pallas_call(functools.partial(kernel, dims), out_shape=(pltpu.VMEM((pa...]
where the time goes in v2:
time: 14.2 us; the launch traced here: 14.1 us
  Pallas kernels  13.4 us (94%)
  between operations  0.64 us (5%)
    pallas_call x1, Pallas kernels, on_device(): pl.pallas_call(functools.partial(kernel, dims), out_shape=(pltpu.VMEM((pa...  12.8 us
    pallas_call x1, Pallas kernels, on_device(): pl.pallas_call(hand_over, out_shape=(jax.ShapeDtypeStruct(tiles.shape, f3...  0.62 us

profile of v2, /device:TPU:0, one launch (start us, length us, event | category | flops | bytes accessed | tf_op | source)
XLA Modules:
  0.0 14.1 jit_solution(11749970280551008906)
XLA Ops:
  0.6 12.8 %shard_map.59 = (f32[2,2,768]{2,1,0:T(2,128)S(1)}, f32[3,8]{1,0:T(4,128)S(1)}) custom-call(f32[2,2,3,64,512]{4,3,2,1,0:T(8,128)} %bitcast.5, f32[2,2,24,3,4,512]{5,4,3,2,1,0:T(4,128)} %bitcast.4, s32[3]{0:T(128)} %times_hbm.1, s32[3,8]{1,0:T(4,128)} %spin_hbm.1), custom_call_target="tpu_custom_call" | custom-call | tf_op jit(solution)/shard_map/pallas_call | solution.py:320
  13.4 0.6 %shard_map.60 = (f32[2,2,768]{2,1,0:T(2,128)}, f32[3,8]{1,0:T(4,128)}) custom-call(f32[2,2,768]{2,1,0:T(2,128)S(1)} %get-tuple-element.4.tiles_ref, f32[3,8]{1,0:T(4,128)S(1)} %get-tuple-element.5.norms_ref), custom_call_target="tpu_custom_call" | custom-call | tf_op jit(solution)/shard_map/pallas_call | solution.py:362

commit v3 on v2

v3 whole, which is shorter than its diff:
```python
import functools
import math

import jax
import jax.numpy as jnp
from jax import lax
from jax.experimental import pallas as pl
from jax.experimental.pallas import tpu as pltpu
from jax.sharding import PartitionSpec as P

LANES = 128
SUBLANES = 8
DIRECT = 64
NT_DIMS = (((1,), (1,)), ((), ()))


def split_two(x):
    high = x.astype(jnp.bfloat16)
    low = (x - high.astype(jnp.float32)).astype(jnp.bfloat16)
    return high, low


def others(count, me):
    for k in range(count - 1):
        past = (me <= k).astype(jnp.int32)
        yield k + past, me - 1 + past


def wait_for(ref, sem):
    pltpu.make_async_copy(ref, ref, sem).wait()


def can_pack(parts, slices, eigs, columns, n_sa):
    return (
        parts == slices == 2 and parts * eigs == LANES
        and 4 * columns == 3 * LANES and eigs % (SUBLANES * n_sa) == 0
    )


def kernel(
    dims,
    eig_hbm, sol_hbm, times_hbm, spin_hbm,
    out_ref, norm_ref,
    eig_buf, sol_buf, eig_split, sol_split, tile_buf, flat_buf,
    send_buf, recv_buf, norm_send, norm_recv,
    times_ref, spin_ref, small_sem,
    eig_sem, sol_sem, out_sem, in_sem, norm_out_sems, norm_in_sems,
):
    n_ta, n_sa, parts, slices, eigs, colors, sites, srcs, cols, spins, width = dims
    columns = srcs * cols * spins
    rows_own = width // LANES
    blocks = sites // LANES
    packed = can_pack(parts, slices, eigs, columns, n_sa)
    pad = LANES - columns
    piece = eigs // n_sa if packed else rows_own
    rows = parts * rows_own
    share = 3 * piece if packed else slices * rows
    sub = math.gcd(share, SUBLANES)
    my_ta, my_sa = lax.axis_index("ta"), lax.axis_index("sa")
    barrier = pltpu.get_barrier_semaphore()

    def flat_device(at):
        return {"ta": lax.div(at, n_sa), "sa": lax.rem(at, n_sa)}

    if n_ta * n_sa <= DIRECT:
        groups = [(n_ta * n_sa, my_ta * n_sa + my_sa, flat_device)]
    else:
        groups = [
            (n_sa, my_sa, lambda at: {"sa": at}),
            (n_ta, my_ta, lambda at: {"ta": at}),
        ]
    chunks = [(t, c) for t in range(slices) for c in range(colors)]

    for t, c in chunks:
        for j in range(blocks):
            at = (t * colors + c) * blocks + j
            pltpu.make_async_copy(
                sol_hbm.at[:, t, :, c, :, pl.ds(j * LANES, LANES)],
                sol_buf.at[at].reshape(parts, srcs * cols, spins, LANES),
                sol_sem.at[t * colors + c],
            ).start()
    for count, me, device in groups:
        for peer, _ in others(count, me):
            pl.semaphore_signal(barrier, inc=1, device_id=device(peer))
    for c in range(colors):
        for t in range(slices):
            pltpu.make_async_copy(
                eig_hbm.at[:, t, c], eig_buf.at[c, t], eig_sem.at[c]
            ).start()
    small_copies = [
        pltpu.make_async_copy(times_hbm, times_ref, small_sem.at[0]),
        pltpu.make_async_copy(spin_hbm, spin_ref, small_sem.at[1]),
    ]
    for copy in small_copies:
        copy.start()

    def sol_blocks(t, c):
        for j in range(blocks):
            lanes = pl.ds(c * sites + j * LANES, LANES)
            for p in range(parts):
                yield p, lanes, sol_buf[(t * colors + c) * blocks + j, p]

    def split_sol(t, c):
        for p, lanes, x in sol_blocks(t, c):
            high, low = split_two(x)
            sol_split[t, pl.ds(p * columns, columns), lanes] = high
            sol_split[t, pl.ds((parts + p) * columns, columns), lanes] = low

    def split_eig(t, c):
        lanes = pl.ds(c * sites, sites)
        for p in range(parts):
            high, low = split_two(eig_buf[c, t, p])
            eig_split[t, pl.ds(p * eigs, eigs), lanes] = high
            eig_split[t, pl.ds((parts + p) * eigs, eigs), lanes] = low

    squares = jnp.zeros((columns, LANES), jnp.float32)
    for t, c in chunks:
        at = t * colors + c
        wait_for(sol_buf.at[pl.ds(at * blocks, blocks)], sol_sem.at[at])
        for _, _, x in sol_blocks(t, c):
            squares = squares + x * x
        if (t, c) != chunks[-1]:
            split_sol(t, c)

    cells = 1.0 * spins * colors * slices * n_ta * sites * n_sa
    sums = jnp.sum(squares, axis=1, keepdims=True) * (1.0 / cells)
    lane = lax.broadcasted_iota(jnp.int32, (columns, LANES), 1)
    group = lax.broadcasted_iota(jnp.int32, (columns, LANES), 0) // spins
    own_norm = jnp.sum(jnp.where(lane == group, sums, 0.0), axis=0, keepdims=True)
    bases = [0, groups[0][0] - 1]

    def send_norm(phase):
        count, me, device = groups[phase]
        for peer, slot in others(count, me):
            pltpu.make_async_remote_copy(
                src_ref=norm_send.at[phase],
                dst_ref=norm_recv.at[bases[phase] + slot],
                send_sem=norm_out_sems.at[phase],
                recv_sem=norm_in_sems.at[phase],
                device_id=device(peer),
            ).start()

    def norm_rows(phase):
        return norm_recv.at[pl.ds(bases[phase], groups[phase][0] - 1)]

    norm_send[0] = own_norm
    last_chip = (2 * my_ta >= n_ta) & (4 * my_sa >= 3 * n_sa)

    def all_here():
        pl.semaphore_wait(barrier, sum(count - 1 for count, _, _ in groups))

    @pl.when(last_chip)
    def _():
        all_here()
        send_norm(0)

    split_sol(*chunks[-1])

    def make_signs(lane_maps):
        for copy in small_copies:
            copy.wait()
        signs = []
        for slice_of, column in lane_maps:
            chir = jnp.ones(column.shape, jnp.float32)
            for s in range(srcs):
                for k in range(cols):
                    value = jnp.where(spin_ref[s, k] < 2, 1.0, -1.0)
                    chir = jnp.where(column // spins == s * cols + k, value, chir)
            now = my_ta * slices + slice_of
            sign = chir
            for s in range(srcs):
                value = jnp.where(now < times_ref[s], -chir, chir)
                sign = jnp.where(column // (spins * cols) == s, value, sign)
            signs.append(sign)
        return signs

    def partial(t, c):
        lanes = pl.ds(c * sites, sites)
        both = lax.dot_general(
            sol_split[t, :, lanes], eig_split[t, :, lanes], NT_DIMS,
            preferred_element_type=jnp.float32,
        )
        return both[: parts * columns] + both[parts * columns :]

    def flatten(t, p, tile):
        period = math.lcm(columns, LANES)
        rows_in, rows_out = period // columns, period // LANES
        count = eigs // rows_in
        lane = lax.broadcasted_iota(jnp.int32, (count, LANES), 1)
        tile_buf[t, p] = tile
        taken = [tile_buf[t, p, pl.ds(i, count, stride=rows_in), :] for i in range(rows_in)]
        for o in range(rows_out):
            value, filled = None, 0
            while filled < LANES:
                i, skip = divmod(o * LANES + filled, columns)
                size = min(columns - skip, LANES - filled)
                shift = (filled - skip) % LANES
                part = pltpu.roll(taken[i], shift, 1) if shift else taken[i]
                value = part if value is None else jnp.where(lane < filled, value, part)
                filled += size
            flat_buf[t, p, pl.ds(o, count, stride=rows_out), :] = value

    def store_flat(totals):
        lane = lax.broadcasted_iota(jnp.int32, (1, LANES), 1)
        signs = make_signs([(jnp.full_like(lane, t), lane) for t in range(slices)])
        for t, g in enumerate(totals):
            real, imag = jnp.transpose(g[:columns]), jnp.transpose(g[columns:])
            tiles = real[:eigs] + imag[eigs:], imag[:eigs] - real[eigs:]
            for p in range(parts):
                tile = tiles[p]
                if pad:
                    tile = jnp.concatenate([tile, jnp.zeros((eigs, pad), jnp.float32)], axis=1)
                flatten(t, p, tile * signs[t])
                for d in range(n_sa):
                    send_buf[pl.ds(d * share + t * rows + p * piece, piece), :] = flat_buf[
                        t, p, pl.ds(d * piece, piece), :
                    ]

    def store_packed(totals):
        first, second = totals
        real0, imag0 = first[:columns], first[columns:]
        real1, imag1 = second[:columns], second[columns:]
        front = lax.broadcasted_iota(jnp.int32, (1, LANES), 1) < eigs
        thirds = [slice(i * pad, (i + 1) * pad) for i in range(3)]

        def turn(body, upper, lower):
            tail = jnp.where(front, upper, lower)
            return jnp.transpose(jnp.concatenate([body, tail], axis=0))

        by_real = turn(real0, imag1[thirds[0]], real1[thirds[1]])
        by_imag = turn(imag0, imag1[thirds[1]], -real1[thirds[0]])
        by_both = turn(jnp.where(front, real1, imag1), imag1[thirds[2]], -real1[thirds[2]])
        tiles = (
            by_real[:eigs] + by_imag[eigs:],
            by_imag[:eigs] - by_real[eigs:],
            by_both[:eigs] + by_both[eigs:],
        )
        for i, tile in enumerate(tiles):
            for d in range(n_sa):
                send_buf[pl.ds(d * share + i * piece, piece), :] = tile[
                    d * piece : (d + 1) * piece
                ]

    def send_tiles():
        sent = send_buf.reshape(n_sa, share // sub, sub, LANES)
        landed = recv_buf.reshape(n_sa - 1, share // sub, sub, LANES)
        for peer, slot in others(n_sa, my_sa):
            pltpu.make_async_remote_copy(
                src_ref=sent.at[peer],
                dst_ref=landed.at[slot],
                send_sem=out_sem,
                recv_sem=in_sem,
                device_id={"sa": peer},
            ).start()

    totals = [None] * slices

    def step(c):
        for t in range(slices):
            both = partial(t, c)
            totals[t] = both if c == 0 else totals[t] + both

    for c in range(colors):
        wait_for(eig_buf.at[c], eig_sem.at[c])
        for t in range(slices):
            split_eig(t, c)
        if c:
            step(c - 1)
    step(colors - 1)
    totals = [g[:, : parts * eigs] + g[:, parts * eigs :] for g in totals]
    store_packed(totals) if packed else store_flat(totals)

    @pl.when(jnp.logical_not(last_chip))
    def _():
        all_here()
        send_norm(0)

    send_tiles()

    if len(groups) > 1:
        wait_for(norm_rows(0), norm_in_sems.at[0])
        own_norm = own_norm + jnp.sum(norm_rows(0)[...], axis=0)
        norm_send[1] = own_norm
        send_norm(1)

    lane = lax.broadcasted_iota(jnp.int32, (SUBLANES, LANES), 1)
    if packed:
        body = lane < columns
        signs = make_signs([
            (jnp.where(body, i // parts, 1), jnp.where(body, lane, lane - columns + i * pad))
            for i in range(3)
        ])
    wait_for(recv_buf, in_sem)
    total = send_buf[pl.ds(my_sa * share, share), :]
    for slot in range(n_sa - 1):
        total = total + recv_buf[pl.ds(slot * share, share), :]

    def join(pieces):
        value = None
        for start, part in pieces:
            value = part if value is None else jnp.where(lane[:1] < start, value, part)
        return value

    def put(t, p, r, value):
        out_ref[p, pl.ds(t, 1), pl.ds(r * LANES, LANES)] = value

    if packed:
        turned = {}
        for i in range(3):
            own = total[i * piece : (i + 1) * piece].reshape(-1, SUBLANES, LANES) * signs[i]
            own = own.reshape(piece, LANES)
            for shift in range(0, LANES, pad):
                turned[i, shift] = pltpu.roll(own, shift, 1) if shift else own
        for r in range(rows_own):
            starts = range(0, LANES, pad)
            from_of = [divmod(r * LANES + start, columns) for start in starts]
            for i in range(3):
                pieces = []
                for start, (row, skip) in zip(starts, from_of):
                    if not start or not skip:
                        pieces.append((start, turned[i, (start - skip) % LANES][row : row + 1]))
                put(i // parts, i % parts, r, join(pieces))
            pieces = [
                (start, turned[skip // pad, (start - columns) % LANES][row : row + 1])
                for start, (row, skip) in zip(starts, from_of)
            ]
            put(1, 1, r, join(pieces))
    else:
        for t in range(slices):
            for p in range(parts):
                for r in range(rows_own):
                    at = t * rows + p * rows_own + r
                    put(t, p, r, total[at : at + 1])
    wait_for(recv_buf, out_sem)
    for phase in range(len(groups)):
        wait_for(norm_rows(phase), norm_out_sems.at[phase])
    final = len(groups) - 1
    wait_for(norm_rows(final), norm_in_sems.at[final])
    own_norm = own_norm + jnp.sum(norm_rows(final)[...], axis=0)
    for s in range(srcs):
        row = pltpu.roll(own_norm, LANES - s * cols, 1) if s else own_norm
        norm_ref[pl.ds(s, 1), :] = row[:, :cols]


def hand_over(tiles_ref, norms_ref, out_hbm, norm_hbm, sems):
    copies = [
        pltpu.make_async_copy(tiles_ref, out_hbm, sems.at[0]),
        pltpu.make_async_copy(norms_ref, norm_hbm, sems.at[1]),
    ]
    for copy in copies:
        copy.start()
    for copy in copies:
        copy.wait()


def on_device(eigvecs, solutions, source_times, spin_dilution):
    n_ta, n_sa = lax.axis_size("ta"), lax.axis_size("sa")
    parts, slices, eigs, colors, sites = eigvecs.shape
    _, _, srcs, cols, spins, _, _ = solutions.shape
    columns = srcs * cols * spins
    width = eigs * columns // n_sa
    eig_view = jnp.transpose(eigvecs, (0, 1, 3, 2, 4))
    sol_view = jnp.transpose(solutions, (0, 1, 2, 3, 5, 4, 6)).reshape(
        parts, slices, srcs * cols, colors, spins, sites
    )
    dims = (n_ta, n_sa, parts, slices, eigs, colors, sites, srcs, cols, spins, width)
    blocks = sites // LANES
    inner = colors * sites
    share = slices * parts * (width // LANES)
    len_groups = 1 if n_ta * n_sa <= DIRECT else 2
    norm_peers = n_ta * n_sa - 1 if n_ta * n_sa <= DIRECT else n_ta + n_sa - 2
    f32, bf16 = jnp.float32, jnp.bfloat16
    dma = pltpu.SemaphoreType.DMA
    tiles, norms = pl.pallas_call(
        functools.partial(kernel, dims),
        out_shape=(
            pltpu.VMEM((parts, slices, width), f32),
            pltpu.VMEM((srcs, cols), f32),
        ),
        in_specs=[
            pl.BlockSpec(memory_space=pltpu.HBM),
            pl.BlockSpec(memory_space=pltpu.HBM),
            pl.BlockSpec(memory_space=pltpu.HBM),
            pl.BlockSpec(memory_space=pltpu.HBM),
        ],
        out_specs=(
            pl.BlockSpec(memory_space=pltpu.VMEM),
            pl.BlockSpec(memory_space=pltpu.VMEM),
        ),
        scratch_shapes=[
            pltpu.VMEM((colors, slices, parts, eigs, sites), f32),
            pltpu.VMEM((slices * colors * blocks, parts, columns, LANES), f32),
            pltpu.VMEM((slices, 2 * parts * eigs, inner), bf16),
            pltpu.VMEM((slices, 2 * parts * columns, inner), bf16),
            pltpu.VMEM((slices, parts, eigs, LANES), f32),
            pltpu.VMEM((slices, parts, eigs * columns // LANES, LANES), f32),
            pltpu.VMEM((n_sa * share, LANES), f32),
            pltpu.VMEM(((n_sa - 1) * share, LANES), f32),
            pltpu.VMEM((2, 1, LANES), f32),
            pltpu.VMEM((norm_peers, 1, LANES), f32),
            pltpu.SMEM((srcs,), jnp.int32),
            pltpu.SMEM((srcs, cols), jnp.int32),
            dma((2,)),
            dma((colors,)),
            dma((slices * colors,)),
            dma,
            dma,
            dma((len_groups,)),
            dma((len_groups,)),
        ],
        compiler_params=pltpu.CompilerParams(
            collective_id=0, has_side_effects=True, vmem_limit_bytes=66 * 10**6
        ),
    )(eig_view, sol_view, source_times, spin_dilution)
    return pl.pallas_call(
        hand_over,
        out_shape=(
            jax.ShapeDtypeStruct(tiles.shape, f32),
            jax.ShapeDtypeStruct(norms.shape, f32),
        ),
        in_specs=[pl.BlockSpec(memory_space=pltpu.VMEM)] * 2,
        out_specs=[pl.BlockSpec(memory_space=pltpu.HBM)] * 2,
        scratch_shapes=[dma((2,))],
        compiler_params=pltpu.CompilerParams(vmem_limit_bytes=2**20),
    )(tiles, norms)


def solution(mesh):
    return jax.shard_map(
        on_device,
        mesh=mesh,
        in_specs=(
            P(None, "ta", None, None, "sa"),
            P(None, "ta", None, None, None, None, "sa"),
            P(),
            P(),
        ),
        out_specs=(P(None, "ta", "sa"), P()),
        check_vma=False,
    )
```

time: 14.2 us -> 12.5 us (0.88)
  Pallas kernels: 13.4 us -> 11.7 us
    pallas_call x1, Pallas kernels: 12.8 us -> 11.1 us  [on_device(): pl.pallas_call(functools.partial(kernel, dims), out_shape=(pltpu.VMEM((pa...]
where the time goes in v3:
time: 12.5 us; the launch traced here: 12.3 us
  Pallas kernels  11.7 us (94%)
  between operations  0.64 us (5%)
    pallas_call x1, Pallas kernels, on_device(): pl.pallas_call(functools.partial(kernel, dims), out_shape=(pltpu.VMEM((pa...  11.1 us
    pallas_call x1, Pallas kernels, on_device(): pl.pallas_call(hand_over, out_shape=(jax.ShapeDtypeStruct(tiles.shape, f3...  0.62 us

profile of v3, /device:TPU:0, one launch (start us, length us, event | category | flops | bytes accessed | tf_op | source)
XLA Modules:
  0.0 12.3 jit_solution(7492707668155542807)
XLA Ops:
  0.6 11.1 %shard_map.59 = (f32[2,2,768]{2,1,0:T(2,128)S(1)}, f32[3,8]{1,0:T(4,128)S(1)}) custom-call(f32[2,2,3,64,512]{4,3,2,1,0:T(8,128)} %bitcast.5, f32[2,2,24,3,4,512]{5,4,3,2,1,0:T(4,128)} %bitcast.4, s32[3]{0:T(128)} %times_hbm.1, s32[3,8]{1,0:T(4,128)} %spin_hbm.1), custom_call_target="tpu_custom_call" | custom-call | tf_op jit(solution)/shard_map/pallas_call | solution.py:374
  11.7 0.6 %shard_map.60 = (f32[2,2,768]{2,1,0:T(2,128)}, f32[3,8]{1,0:T(4,128)}) custom-call(f32[2,2,768]{2,1,0:T(2,128)S(1)} %get-tuple-element.4.tiles_ref, f32[3,8]{1,0:T(4,128)S(1)} %get-tuple-element.5.norms_ref), custom_call_target="tpu_custom_call" | custom-call | tf_op jit(solution)/shard_map/pallas_call | solution.py:415

commit v4 on v3

--- a/solution.py
+++ b/solution.py
@@ -71,7 +71,7 @@
         ]
     chunks = [(t, c) for t in range(slices) for c in range(colors)]
 
-    for t, c in chunks:
+    def read_sol(t, c):
         for j in range(blocks):
             at = (t * colors + c) * blocks + j
             pltpu.make_async_copy(
@@ -79,9 +79,15 @@
                 sol_buf.at[at].reshape(parts, srcs * cols, spins, LANES),
                 sol_sem.at[t * colors + c],
             ).start()
+
+    ahead = len(chunks) // 2
+    for t, c in chunks[:ahead]:
+        read_sol(t, c)
     for count, me, device in groups:
         for peer, _ in others(count, me):
             pl.semaphore_signal(barrier, inc=1, device_id=device(peer))
+    for t, c in chunks[ahead:]:
+        read_sol(t, c)
     for c in range(colors):
         for t in range(slices):
             pltpu.make_async_copy(
@@ -127,32 +133,40 @@
     lane = lax.broadcasted_iota(jnp.int32, (columns, LANES), 1)
     group = lax.broadcasted_iota(jnp.int32, (columns, LANES), 0) // spins
     own_norm = jnp.sum(jnp.where(lane == group, sums, 0.0), axis=0, keepdims=True)
-    bases = [0, groups[0][0] - 1]
-
-    def send_norm(phase):
+
+    def norm_rows(phase):
+        count = groups[phase][0]
+        return norm_recv.at[phase].reshape(norm_recv.shape[1], 1, LANES).at[pl.ds(0, count - 1)]
+
+    def send_norm(phase, begin, end):
         count, me, device = groups[phase]
-        for peer, slot in others(count, me):
+        rows_there = norm_recv.at[phase].reshape(norm_recv.shape[1], 1, LANES)
+        for peer, slot in list(others(count, me))[begin:end]:
             pltpu.make_async_remote_copy(
                 src_ref=norm_send.at[phase],
-                dst_ref=norm_recv.at[bases[phase] + slot],
+                dst_ref=rows_there.at[slot],
                 send_sem=norm_out_sems.at[phase],
                 recv_sem=norm_in_sems.at[phase],
                 device_id=device(peer),
             ).start()
 
-    def norm_rows(phase):
-        return norm_recv.at[pl.ds(bases[phase], groups[phase][0] - 1)]
-
-    norm_send[0] = own_norm
-    last_chip = (2 * my_ta >= n_ta) & (4 * my_sa >= 3 * n_sa)
+    def put_norm(phase, row):
+        count = groups[phase][0]
+        norm_send[phase] = row
+        norm_recv[phase, pl.ds(count - 1, 1), :] = row
+        for at in range(count, norm_recv.shape[1]):
+            norm_recv[phase, pl.ds(at, 1), :] = jnp.zeros((1, LANES), jnp.float32)
 
     def all_here():
         pl.semaphore_wait(barrier, sum(count - 1 for count, _, _ in groups))
 
-    @pl.when(last_chip)
+    put_norm(0, own_norm)
+    norm_first = my_ta > 0
+
+    @pl.when(norm_first)
     def _():
         all_here()
-        send_norm(0)
+        send_norm(0, 0, None)
 
     split_sol(*chunks[-1])
 
@@ -241,10 +255,10 @@
                     d * piece : (d + 1) * piece
                 ]
 
-    def send_tiles():
+    def send_tiles(begin, end):
         sent = send_buf.reshape(n_sa, share // sub, sub, LANES)
         landed = recv_buf.reshape(n_sa - 1, share // sub, sub, LANES)
-        for peer, slot in others(n_sa, my_sa):
+        for peer, slot in list(others(n_sa, my_sa))[begin:end]:
             pltpu.make_async_remote_copy(
                 src_ref=sent.at[peer],
                 dst_ref=landed.at[slot],
@@ -260,28 +274,36 @@
             both = partial(t, c)
             totals[t] = both if c == 0 else totals[t] + both
 
+    wait_for(eig_buf.at[0], eig_sem.at[0])
+    for t in range(slices):
+        split_eig(t, 0)
+    for c in range(1, colors):
+        wait_for(eig_buf.at[c], eig_sem.at[c])
     for c in range(colors):
-        wait_for(eig_buf.at[c], eig_sem.at[c])
-        for t in range(slices):
-            split_eig(t, c)
         if c:
-            step(c - 1)
-    step(colors - 1)
+            for t in range(slices):
+                split_eig(t, c)
+        step(c)
     totals = [g[:, : parts * eigs] + g[:, parts * eigs :] for g in totals]
     store_packed(totals) if packed else store_flat(totals)
 
-    @pl.when(jnp.logical_not(last_chip))
+    @pl.when(jnp.logical_not(norm_first))
     def _():
         all_here()
-        send_norm(0)
-
-    send_tiles()
+        send_norm(0, 0, 2)
+        send_tiles(0, 2)
+        send_norm(0, 2, None)
+
+    @pl.when(norm_first)
+    def _():
+        send_tiles(0, 2)
+
+    send_tiles(2, None)
 
     if len(groups) > 1:
         wait_for(norm_rows(0), norm_in_sems.at[0])
-        own_norm = own_norm + jnp.sum(norm_rows(0)[...], axis=0)
-        norm_send[1] = own_norm
-        send_norm(1)
+        put_norm(1, jnp.sum(norm_recv[0], axis=0, keepdims=True))
+        send_norm(1, 0, None)
 
     lane = lax.broadcasted_iota(jnp.int32, (SUBLANES, LANES), 1)
     if packed:
@@ -336,9 +358,9 @@
         wait_for(norm_rows(phase), norm_out_sems.at[phase])
     final = len(groups) - 1
     wait_for(norm_rows(final), norm_in_sems.at[final])
-    own_norm = own_norm + jnp.sum(norm_rows(final)[...], axis=0)
+    norm = jnp.sum(norm_recv[final], axis=0, keepdims=True)
     for s in range(srcs):
-        row = pltpu.roll(own_norm, LANES - s * cols, 1) if s else own_norm
+        row = pltpu.roll(norm, LANES - s * cols, 1) if s else norm
         norm_ref[pl.ds(s, 1), :] = row[:, :cols]
 
 
@@ -368,7 +390,8 @@
     inner = colors * sites
     share = slices * parts * (width // LANES)
     len_groups = 1 if n_ta * n_sa <= DIRECT else 2
-    norm_peers = n_ta * n_sa - 1 if n_ta * n_sa <= DIRECT else n_ta + n_sa - 2
+    most = n_ta * n_sa if n_ta * n_sa <= DIRECT else max(n_ta, n_sa)
+    norm_rows = pl.cdiv(most, SUBLANES) * SUBLANES
     f32, bf16 = jnp.float32, jnp.bfloat16
     dma = pltpu.SemaphoreType.DMA
     tiles, norms = pl.pallas_call(
@@ -396,8 +419,8 @@
             pltpu.VMEM((slices, parts, eigs * columns // LANES, LANES), f32),
             pltpu.VMEM((n_sa * share, LANES), f32),
             pltpu.VMEM(((n_sa - 1) * share, LANES), f32),
-            pltpu.VMEM((2, 1, LANES), f32),
-            pltpu.VMEM((norm_peers, 1, LANES), f32),
+            pltpu.VMEM((len_groups, 1, LANES), f32),
+            pltpu.VMEM((len_groups, norm_rows, LANES), f32),
             pltpu.SMEM((srcs,), jnp.int32),
             pltpu.SMEM((srcs, cols), jnp.int32),
             dma((2,)),

time: 12.5 us -> 12.3 us (0.984)
  Pallas kernels: 11.7 us -> 11.5 us
    pallas_call x1, Pallas kernels: 11.1 us -> 10.9 us  [on_device(): pl.pallas_call(functools.partial(kernel, dims), out_shape=(pltpu.VMEM((pa...]
where the time goes in v4:
time: 12.3 us; the launch traced here: 12.2 us
  Pallas kernels  11.5 us (93%)
  between operations  0.64 us (5%)
    pallas_call x1, Pallas kernels, on_device(): pl.pallas_call(functools.partial(kernel, dims), out_shape=(pltpu.VMEM((pa...  10.9 us
    pallas_call x1, Pallas kernels, on_device(): pl.pallas_call(hand_over, out_shape=(jax.ShapeDtypeStruct(tiles.shape, f3...  0.62 us

profile of v4, /device:TPU:0, one launch (start us, length us, event | category | flops | bytes accessed | tf_op | source)
XLA Modules:
  0.0 12.2 jit_solution(9549867985172248318)
XLA Ops:
  0.6 10.9 %shard_map.59 = (f32[2,2,768]{2,1,0:T(2,128)S(1)}, f32[3,8]{1,0:T(4,128)S(1)}) custom-call(f32[2,2,3,64,512]{4,3,2,1,0:T(8,128)} %bitcast.5, f32[2,2,24,3,4,512]{5,4,3,2,1,0:T(4,128)} %bitcast.4, s32[3]{0:T(128)} %times_hbm.1, s32[3,8]{1,0:T(4,128)} %spin_hbm.1), custom_call_target="tpu_custom_call" | custom-call | tf_op jit(solution)/shard_map/pallas_call | solution.py:397
  11.5 0.6 %shard_map.60 = (f32[2,2,768]{2,1,0:T(2,128)}, f32[3,8]{1,0:T(4,128)}) custom-call(f32[2,2,768]{2,1,0:T(2,128)S(1)} %get-tuple-element.4.tiles_ref, f32[3,8]{1,0:T(4,128)S(1)} %get-tuple-element.5.norms_ref), custom_call_target="tpu_custom_call" | custom-call | tf_op jit(solution)/shard_map/pallas_call | solution.py:438

commit v5 on v4

--- a/solution.py
+++ b/solution.py
@@ -41,10 +41,10 @@
     dims,
     eig_hbm, sol_hbm, times_hbm, spin_hbm,
     out_ref, norm_ref,
-    eig_buf, sol_buf, eig_split, sol_split, tile_buf, flat_buf,
+    eig_buf, sol_buf, eig_split, sol_split, g_buf, tile_buf, flat_buf,
     send_buf, recv_buf, norm_send, norm_recv,
     times_ref, spin_ref, small_sem,
-    eig_sem, sol_sem, out_sem, in_sem, norm_out_sems, norm_in_sems,
+    eig_sem, sol_sem, out_sems, in_sem, norm_out_sems, norm_in_sems,
 ):
     n_ta, n_sa, parts, slices, eigs, colors, sites, srcs, cols, spins, width = dims
     columns = srcs * cols * spins
@@ -71,14 +71,15 @@
         ]
     chunks = [(t, c) for t in range(slices) for c in range(colors)]
 
+    nodes = srcs * cols
+    gap = (blocks + 1) * spins
+
     def read_sol(t, c):
-        for j in range(blocks):
-            at = (t * colors + c) * blocks + j
-            pltpu.make_async_copy(
-                sol_hbm.at[:, t, :, c, :, pl.ds(j * LANES, LANES)],
-                sol_buf.at[at].reshape(parts, srcs * cols, spins, LANES),
-                sol_sem.at[t * colors + c],
-            ).start()
+        at = t * colors + c
+        into = sol_buf.at[at].reshape(parts, nodes, blocks + 1, spins, LANES)
+        pltpu.make_async_copy(
+            sol_hbm.at[:, t, :, c], into.at[:, :, pl.ds(0, blocks)], sol_sem.at[at]
+        ).start()
 
     ahead = len(chunks) // 2
     for t, c in chunks[:ahead]:
@@ -101,16 +102,30 @@
         copy.start()
 
     def sol_blocks(t, c):
+        at = t * colors + c
         for j in range(blocks):
             lanes = pl.ds(c * sites + j * LANES, LANES)
             for p in range(parts):
-                yield p, lanes, sol_buf[(t * colors + c) * blocks + j, p]
+                x = [
+                    sol_buf[at, p, pl.ds(j * spins + spin, nodes, stride=gap), :]
+                    for spin in range(spins)
+                ]
+                yield p, lanes, jnp.concatenate(x, axis=0)
 
     def split_sol(t, c):
         for p, lanes, x in sol_blocks(t, c):
             high, low = split_two(x)
             sol_split[t, pl.ds(p * columns, columns), lanes] = high
             sol_split[t, pl.ds((parts + p) * columns, columns), lanes] = low
+
+    def by_column(t, g):
+        for p in range(parts):
+            for spin in range(spins):
+                start = (p * spins + spin) * nodes
+                g_buf[t, pl.ds(p * columns + spin, nodes, stride=spins), :] = g[
+                    start : start + nodes
+                ]
+        return g_buf[t]
 
     def split_eig(t, c):
         lanes = pl.ds(c * sites, sites)
@@ -122,17 +137,19 @@
     squares = jnp.zeros((columns, LANES), jnp.float32)
     for t, c in chunks:
         at = t * colors + c
-        wait_for(sol_buf.at[pl.ds(at * blocks, blocks)], sol_sem.at[at])
+        into = sol_buf.at[at].reshape(parts, nodes, blocks + 1, spins, LANES)
+        wait_for(into.at[:, :, pl.ds(0, blocks)], sol_sem.at[at])
         for _, _, x in sol_blocks(t, c):
             squares = squares + x * x
         if (t, c) != chunks[-1]:
             split_sol(t, c)
 
     cells = 1.0 * spins * colors * slices * n_ta * sites * n_sa
+    squares = sum(squares[spin * nodes : (spin + 1) * nodes] for spin in range(spins))
     sums = jnp.sum(squares, axis=1, keepdims=True) * (1.0 / cells)
-    lane = lax.broadcasted_iota(jnp.int32, (columns, LANES), 1)
-    group = lax.broadcasted_iota(jnp.int32, (columns, LANES), 0) // spins
-    own_norm = jnp.sum(jnp.where(lane == group, sums, 0.0), axis=0, keepdims=True)
+    lane = lax.broadcasted_iota(jnp.int32, (nodes, LANES), 1)
+    node = lax.broadcasted_iota(jnp.int32, (nodes, LANES), 0)
+    own_norm = jnp.sum(jnp.where(lane == node, sums, 0.0), axis=0, keepdims=True)
 
     def norm_rows(phase):
         count = groups[phase][0]
@@ -262,10 +279,13 @@
             pltpu.make_async_remote_copy(
                 src_ref=sent.at[peer],
                 dst_ref=landed.at[slot],
-                send_sem=out_sem,
+                send_sem=out_sems.at[min(begin, 1)],
                 recv_sem=in_sem,
                 device_id={"sa": peer},
             ).start()
+
+    def first_sent():
+        wait_for(recv_buf.at[pl.ds(0, 2 * share)], out_sems.at[0])
 
     totals = [None] * slices
 
@@ -284,7 +304,9 @@
             for t in range(slices):
                 split_eig(t, c)
         step(c)
-    totals = [g[:, : parts * eigs] + g[:, parts * eigs :] for g in totals]
+    totals = [
+        by_column(t, g[:, : parts * eigs] + g[:, parts * eigs :]) for t, g in enumerate(totals)
+    ]
     store_packed(totals) if packed else store_flat(totals)
 
     @pl.when(jnp.logical_not(norm_first))
@@ -293,10 +315,12 @@
         send_norm(0, 0, 2)
         send_tiles(0, 2)
         send_norm(0, 2, None)
+        first_sent()
 
     @pl.when(norm_first)
     def _():
         send_tiles(0, 2)
+        first_sent()
 
     send_tiles(2, None)
 
@@ -353,7 +377,7 @@
                 for r in range(rows_own):
                     at = t * rows + p * rows_own + r
                     put(t, p, r, total[at : at + 1])
-    wait_for(recv_buf, out_sem)
+    wait_for(recv_buf.at[pl.ds(2 * share, (n_sa - 3) * share)], out_sems.at[1])
     for phase in range(len(groups)):
         wait_for(norm_rows(phase), norm_out_sems.at[phase])
     final = len(groups) - 1
@@ -382,8 +406,9 @@
     columns = srcs * cols * spins
     width = eigs * columns // n_sa
     eig_view = jnp.transpose(eigvecs, (0, 1, 3, 2, 4))
-    sol_view = jnp.transpose(solutions, (0, 1, 2, 3, 5, 4, 6)).reshape(
-        parts, slices, srcs * cols, colors, spins, sites
+    sol_view = jnp.transpose(
+        solutions.reshape(parts, slices, srcs * cols, spins, colors, sites // LANES, LANES),
+        (0, 1, 2, 4, 5, 3, 6),
     )
     dims = (n_ta, n_sa, parts, slices, eigs, colors, sites, srcs, cols, spins, width)
     blocks = sites // LANES
@@ -412,9 +437,10 @@
         ),
         scratch_shapes=[
             pltpu.VMEM((colors, slices, parts, eigs, sites), f32),
-            pltpu.VMEM((slices * colors * blocks, parts, columns, LANES), f32),
+            pltpu.VMEM((slices * colors, parts, columns * (blocks + 1), LANES), f32),
             pltpu.VMEM((slices, 2 * parts * eigs, inner), bf16),
             pltpu.VMEM((slices, 2 * parts * columns, inner), bf16),
+            pltpu.VMEM((slices, parts * columns, parts * eigs), f32),
             pltpu.VMEM((slices, parts, eigs, LANES), f32),
             pltpu.VMEM((slices, parts, eigs * columns // LANES, LANES), f32),
             pltpu.VMEM((n_sa * share, LANES), f32),
@@ -426,7 +452,7 @@
             dma((2,)),
             dma((colors,)),
             dma((slices * colors,)),
-            dma,
+            dma((2,)),
             dma,
             dma((len_groups,)),
             dma((len_groups,)),

time: 12.3 us -> 12 us (0.976)
  Pallas kernels: 11.5 us -> 11.2 us
    pallas_call x1, Pallas kernels: 10.9 us -> 10.5 us  [on_device(): pl.pallas_call(functools.partial(kernel, dims), out_shape=(pltpu.VMEM((pa...]
where the time goes in v5:
time: 12 us; the launch traced here: 11.8 us
  Pallas kernels  11.2 us (93%)
  between operations  0.64 us (5%)
    pallas_call x1, Pallas kernels, on_device(): pl.pallas_call(functools.partial(kernel, dims), out_shape=(pltpu.VMEM((pa...  10.5 us
    pallas_call x1, Pallas kernels, on_device(): pl.pallas_call(hand_over, out_shape=(jax.ShapeDtypeStruct(tiles.shape, f3...  0.62 us

profile of v5, /device:TPU:0, one launch (start us, length us, event | category | flops | bytes accessed | tf_op | source)
XLA Modules:
  0.0 11.8 jit_solution(14136264337288325993)
XLA Ops:
  0.6 10.5 %shard_map.59 = (f32[2,2,768]{2,1,0:T(2,128)S(1)}, f32[3,8]{1,0:T(4,128)S(1)}) custom-call(f32[2,2,3,64,512]{4,3,2,1,0:T(8,128)} %bitcast.5, f32[2,2,24,3,4,4,128]{6,5,4,3,2,1,0:T(4,128)} %bitcast.4, s32[3]{0:T(128)} %times_hbm.1, s32[3,8]{1,0:T(4,128)} %spin_hbm.1), custom_call_target="tpu_custom_call" | custom-call | tf_op jit(solution)/shard_map/pallas_call | solution.py:422
  11.2 0.6 %shard_map.60 = (f32[2,2,768]{2,1,0:T(2,128)}, f32[3,8]{1,0:T(4,128)}) custom-call(f32[2,2,768]{2,1,0:T(2,128)S(1)} %get-tuple-element.4.tiles_ref, f32[3,8]{1,0:T(4,128)S(1)} %get-tuple-element.5.norms_ref), custom_call_target="tpu_custom_call" | custom-call | tf_op jit(solution)/shard_map/pallas_call | solution.py:464

commit v6 on v5

--- a/solution.py
+++ b/solution.py
@@ -11,6 +11,7 @@
 LANES = 128
 SUBLANES = 8
 DIRECT = 64
+HUBS = 2
 NT_DIMS = (((1,), (1,)), ((), ()))
 
 
@@ -44,7 +45,7 @@
     eig_buf, sol_buf, eig_split, sol_split, g_buf, tile_buf, flat_buf,
     send_buf, recv_buf, norm_send, norm_recv,
     times_ref, spin_ref, small_sem,
-    eig_sem, sol_sem, out_sems, in_sem, norm_out_sems, norm_in_sems,
+    eig_sem, sol_sem, out_sems, in_sem, norm_out_sems, norm_in_sems, line_sem,
 ):
     n_ta, n_sa, parts, slices, eigs, colors, sites, srcs, cols, spins, width = dims
     columns = srcs * cols * spins
@@ -62,13 +63,12 @@
     def flat_device(at):
         return {"ta": lax.div(at, n_sa), "sa": lax.rem(at, n_sa)}
 
-    if n_ta * n_sa <= DIRECT:
-        groups = [(n_ta * n_sa, my_ta * n_sa + my_sa, flat_device)]
-    else:
-        groups = [
-            (n_sa, my_sa, lambda at: {"sa": at}),
-            (n_ta, my_ta, lambda at: {"ta": at}),
-        ]
+    direct = n_ta * n_sa <= DIRECT
+    lines = [
+        (n_sa, my_sa, lambda at: {"sa": at}),
+        (n_ta, my_ta, lambda at: {"ta": at}),
+    ]
+    groups = [(n_ta * n_sa, my_ta * n_sa + my_sa, flat_device)] if direct else lines
     chunks = [(t, c) for t in range(slices) for c in range(colors)]
 
     nodes = srcs * cols
@@ -84,7 +84,7 @@
     ahead = len(chunks) // 2
     for t, c in chunks[:ahead]:
         read_sol(t, c)
-    for count, me, device in groups:
+    for count, me, device in lines:
         for peer, _ in others(count, me):
             pl.semaphore_signal(barrier, inc=1, device_id=device(peer))
     for t, c in chunks[ahead:]:
@@ -101,6 +101,17 @@
     for copy in small_copies:
         copy.start()
 
+    expected = n_sa - 1 + n_ta - 1
+    if direct:
+        @pl.when((my_ta == 0) & (my_sa < HUBS))
+        def _():
+            for a in range(1, n_ta):
+                for peer, _ in others(n_sa, my_sa):
+                    pl.semaphore_signal(barrier, inc=1, device_id={"ta": a, "sa": peer})
+
+        far_hubs = HUBS - (my_sa < HUBS).astype(jnp.int32)
+        expected = expected + jnp.where(my_ta > 0, far_hubs, 0)
+
     def sol_blocks(t, c):
         at = t * colors + c
         for j in range(blocks):
@@ -174,16 +185,26 @@
         for at in range(count, norm_recv.shape[1]):
             norm_recv[phase, pl.ds(at, 1), :] = jnp.zeros((1, LANES), jnp.float32)
 
+    def lines_here():
+        pl.semaphore_wait(barrier, expected)
+        send_norm(0, 0, HUBS)
+
+    def tell_line():
+        if direct:
+            for peer, _ in others(n_ta, my_ta):
+                pl.semaphore_signal(line_sem, inc=1, device_id={"ta": peer})
+
     def all_here():
-        pl.semaphore_wait(barrier, sum(count - 1 for count, _, _ in groups))
+        if direct:
+            pl.semaphore_wait(line_sem, n_ta - 1)
 
     put_norm(0, own_norm)
     norm_first = my_ta > 0
 
     @pl.when(norm_first)
     def _():
-        all_here()
-        send_norm(0, 0, None)
+        lines_here()
+        tell_line()
 
     split_sol(*chunks[-1])
 
@@ -311,17 +332,17 @@
 
     @pl.when(jnp.logical_not(norm_first))
     def _():
-        all_here()
-        send_norm(0, 0, 2)
-        send_tiles(0, 2)
-        send_norm(0, 2, None)
-        first_sent()
-
-    @pl.when(norm_first)
+        lines_here()
+
+    send_tiles(0, 2)
+
+    @pl.when(jnp.logical_not(norm_first))
     def _():
-        send_tiles(0, 2)
-        first_sent()
-
+        tell_line()
+
+    all_here()
+    send_norm(0, HUBS, None)
+    first_sent()
     send_tiles(2, None)
 
     if len(groups) > 1:
@@ -456,6 +477,7 @@
             dma,
             dma((len_groups,)),
             dma((len_groups,)),
+            pltpu.SemaphoreType.REGULAR,
         ],
         compiler_params=pltpu.CompilerParams(
             collective_id=0, has_side_effects=True, vmem_limit_bytes=66 * 10**6

time: 12 us -> 11.9 us (level)
  no operation moved by 1% of the time
where the time goes in v6:
time: 11.9 us; the launch traced here: 11.8 us
  Pallas kernels  11.1 us (93%)
  between operations  0.64 us (5%)
    pallas_call x1, Pallas kernels, on_device(): pl.pallas_call(functools.partial(kernel, dims), out_shape=(pltpu.VMEM((pa...  10.5 us
    pallas_call x1, Pallas kernels, on_device(): pl.pallas_call(hand_over, out_shape=(jax.ShapeDtypeStruct(tiles.shape, f3...  0.62 us

profile of v6, /device:TPU:0, one launch (start us, length us, event | category | flops | bytes accessed | tf_op | source)
XLA Modules:
  0.0 11.8 jit_solution(17695228271056097494)
XLA Ops:
  0.6 10.5 %shard_map.59 = (f32[2,2,768]{2,1,0:T(2,128)S(1)}, f32[3,8]{1,0:T(4,128)S(1)}) custom-call(f32[2,2,3,64,512]{4,3,2,1,0:T(8,128)} %bitcast.5, f32[2,2,24,3,4,4,128]{6,5,4,3,2,1,0:T(4,128)} %bitcast.4, s32[3]{0:T(128)} %times_hbm.1, s32[3,8]{1,0:T(4,128)} %spin_hbm.1), custom_call_target="tpu_custom_call" | custom-call | tf_op jit(solution)/shard_map/pallas_call | solution.py:443
  11.2 0.6 %shard_map.60 = (f32[2,2,768]{2,1,0:T(2,128)}, f32[3,8]{1,0:T(4,128)}) custom-call(f32[2,2,768]{2,1,0:T(2,128)S(1)} %get-tuple-element.4.tiles_ref, f32[3,8]{1,0:T(4,128)S(1)} %get-tuple-element.5.norms_ref), custom_call_target="tpu_custom_call" | custom-call | tf_op jit(solution)/shard_map/pallas_call | solution.py:486

commit v7 on v6

--- a/solution.py
+++ b/solution.py
@@ -92,7 +92,7 @@
     for c in range(colors):
         for t in range(slices):
             pltpu.make_async_copy(
-                eig_hbm.at[:, t, c], eig_buf.at[c, t], eig_sem.at[c]
+                eig_hbm.at[:, t, c], eig_buf.at[c, t], eig_sem.at[min(c, 1)]
             ).start()
     small_copies = [
         pltpu.make_async_copy(times_hbm, times_ref, small_sem.at[0]),
@@ -318,8 +318,7 @@
     wait_for(eig_buf.at[0], eig_sem.at[0])
     for t in range(slices):
         split_eig(t, 0)
-    for c in range(1, colors):
-        wait_for(eig_buf.at[c], eig_sem.at[c])
+    wait_for(eig_buf.at[pl.ds(1, colors - 1)], eig_sem.at[1])
     for c in range(colors):
         if c:
             for t in range(slices):
@@ -403,21 +402,22 @@
         wait_for(norm_rows(phase), norm_out_sems.at[phase])
     final = len(groups) - 1
     wait_for(norm_rows(final), norm_in_sems.at[final])
-    norm = jnp.sum(norm_recv[final], axis=0, keepdims=True)
+    rows_by_vreg = norm_recv[final].reshape(-1, SUBLANES, LANES)
+    norm_ref[...] = jnp.sum(rows_by_vreg, axis=0)
+
+
+def hand_over(tiles_ref, norms_ref, out_hbm, norm_hbm, norm_buf, sems):
+    tile_copy = pltpu.make_async_copy(tiles_ref, out_hbm, sems.at[0])
+    tile_copy.start()
+    srcs, cols = norm_buf.shape
+    norm = jnp.sum(norms_ref[...], axis=0, keepdims=True)
     for s in range(srcs):
         row = pltpu.roll(norm, LANES - s * cols, 1) if s else norm
-        norm_ref[pl.ds(s, 1), :] = row[:, :cols]
-
-
-def hand_over(tiles_ref, norms_ref, out_hbm, norm_hbm, sems):
-    copies = [
-        pltpu.make_async_copy(tiles_ref, out_hbm, sems.at[0]),
-        pltpu.make_async_copy(norms_ref, norm_hbm, sems.at[1]),
-    ]
-    for copy in copies:
-        copy.start()
-    for copy in copies:
-        copy.wait()
+        norm_buf[pl.ds(s, 1), :] = row[:, :cols]
+    norm_copy = pltpu.make_async_copy(norm_buf, norm_hbm, sems.at[1])
+    norm_copy.start()
+    tile_copy.wait()
+    norm_copy.wait()
 
 
 def on_device(eigvecs, solutions, source_times, spin_dilution):
@@ -444,7 +444,7 @@
         functools.partial(kernel, dims),
         out_shape=(
             pltpu.VMEM((parts, slices, width), f32),
-            pltpu.VMEM((srcs, cols), f32),
+            pltpu.VMEM((SUBLANES, LANES), f32),
         ),
         in_specs=[
             pl.BlockSpec(memory_space=pltpu.HBM),
@@ -471,7 +471,7 @@
             pltpu.SMEM((srcs,), jnp.int32),
             pltpu.SMEM((srcs, cols), jnp.int32),
             dma((2,)),
-            dma((colors,)),
+            dma((2,)),
             dma((slices * colors,)),
             dma((2,)),
             dma,
@@ -487,11 +487,11 @@
         hand_over,
         out_shape=(
             jax.ShapeDtypeStruct(tiles.shape, f32),
-            jax.ShapeDtypeStruct(norms.shape, f32),
+            jax.ShapeDtypeStruct((srcs, cols), f32),
         ),
         in_specs=[pl.BlockSpec(memory_space=pltpu.VMEM)] * 2,
         out_specs=[pl.BlockSpec(memory_space=pltpu.HBM)] * 2,
-        scratch_shapes=[dma((2,))],
+        scratch_shapes=[pltpu.VMEM((srcs, cols), f32), dma((2,))],
         compiler_params=pltpu.CompilerParams(vmem_limit_bytes=2**20),
     )(tiles, norms)
 

time: 11.9 us -> 11.9 us (level)
  no operation moved by 1% of the time
where the time goes in v7:
time: 11.9 us; the launch traced here: 11.7 us
  Pallas kernels  11.1 us (93%)
  between operations  0.64 us (5%)
    pallas_call x1, Pallas kernels, on_device(): pl.pallas_call(functools.partial(kernel, dims), out_shape=(pltpu.VMEM((pa...  10.4 us
    pallas_call x1, Pallas kernels, on_device(): pl.pallas_call(hand_over, out_shape=(jax.ShapeDtypeStruct(tiles.shape, f3...  0.66 us

profile of v7, /device:TPU:0, one launch (start us, length us, event | category | flops | bytes accessed | tf_op | source)
XLA Modules:
  0.0 11.7 jit_solution(12701016034745943238)
XLA Ops:
  0.6 10.4 %shard_map.59 = (f32[2,2,768]{2,1,0:T(2,128)S(1)}, f32[8,128]{1,0:T(8,128)S(1)}) custom-call(f32[2,2,3,64,512]{4,3,2,1,0:T(8,128)} %bitcast.5, f32[2,2,24,3,4,4,128]{6,5,4,3,2,1,0:T(4,128)} %bitcast.4, s32[3]{0:T(128)} %times_hbm.1, s32[3,8]{1,0:T(4,128)} %spin_hbm.1), custom_call_target="tpu_custom_call" | custom-call | tf_op jit(solution)/shard_map/pallas_call | solution.py:443
  11.1 0.7 %shard_map.60 = (f32[2,2,768]{2,1,0:T(2,128)}, f32[3,8]{1,0:T(4,128)}) custom-call(f32[2,2,768]{2,1,0:T(2,128)S(1)} %get-tuple-element.4.tiles_ref, f32[8,128]{1,0:T(8,128)S(1)} %get-tuple-element.5.norms_ref), custom_call_target="tpu_custom_call" | custom-call | tf_op jit(solution)/shard_map/pallas_call | solution.py:486

commit v8 on v7

--- a/solution.py
+++ b/solution.py
@@ -12,6 +12,7 @@
 SUBLANES = 8
 DIRECT = 64
 HUBS = 2
+LATE_SPLITS = 3
 NT_DIMS = (((1,), (1,)), ((), ()))
 
 
@@ -152,7 +153,7 @@
         wait_for(into.at[:, :, pl.ds(0, blocks)], sol_sem.at[at])
         for _, _, x in sol_blocks(t, c):
             squares = squares + x * x
-        if (t, c) != chunks[-1]:
+        if (t, c) not in chunks[-LATE_SPLITS:]:
             split_sol(t, c)
 
     cells = 1.0 * spins * colors * slices * n_ta * sites * n_sa
@@ -206,7 +207,8 @@
         lines_here()
         tell_line()
 
-    split_sol(*chunks[-1])
+    for t, c in chunks[-LATE_SPLITS:]:
+        split_sol(t, c)
 
     def make_signs(lane_maps):
         for copy in small_copies:

time: 11.9 us -> 11.9 us (level)
  no operation moved by 1% of the time
where the time goes in v8:
time: 11.9 us; the launch traced here: 11.7 us
  Pallas kernels  11.1 us (93%)
  between operations  0.64 us (5%)
    pallas_call x1, Pallas kernels, on_device(): pl.pallas_call(functools.partial(kernel, dims), out_shape=(pltpu.VMEM((pa...  10.4 us
    pallas_call x1, Pallas kernels, on_device(): pl.pallas_call(hand_over, out_shape=(jax.ShapeDtypeStruct(tiles.shape, f3...  0.66 us

profile of v8, /device:TPU:0, one launch (start us, length us, event | category | flops | bytes accessed | tf_op | source)
XLA Modules:
  0.0 11.7 jit_solution(377368741062816218)
XLA Ops:
  0.6 10.4 %shard_map.59 = (f32[2,2,768]{2,1,0:T(2,128)S(1)}, f32[8,128]{1,0:T(8,128)S(1)}) custom-call(f32[2,2,3,64,512]{4,3,2,1,0:T(8,128)} %bitcast.5, f32[2,2,24,3,4,4,128]{6,5,4,3,2,1,0:T(4,128)} %bitcast.4, s32[3]{0:T(128)} %times_hbm.1, s32[3,8]{1,0:T(4,128)} %spin_hbm.1), custom_call_target="tpu_custom_call" | custom-call | tf_op jit(solution)/shard_map/pallas_call | solution.py:445
  11.1 0.7 %shard_map.60 = (f32[2,2,768]{2,1,0:T(2,128)}, f32[3,8]{1,0:T(4,128)}) custom-call(f32[2,2,768]{2,1,0:T(2,128)S(1)} %get-tuple-element.4.tiles_ref, f32[8,128]{1,0:T(8,128)S(1)} %get-tuple-element.5.norms_ref), custom_call_target="tpu_custom_call" | custom-call | tf_op jit(solution)/shard_map/pallas_call | solution.py:488

commit v9 on v8

--- a/solution.py
+++ b/solution.py
@@ -12,7 +12,7 @@
 SUBLANES = 8
 DIRECT = 64
 HUBS = 2
-LATE_SPLITS = 3
+LATE_SPLITS = 4
 NT_DIMS = (((1,), (1,)), ((), ()))
 
 
@@ -82,7 +82,7 @@
             sol_hbm.at[:, t, :, c], into.at[:, :, pl.ds(0, blocks)], sol_sem.at[at]
         ).start()
 
-    ahead = len(chunks) // 2
+    ahead = len(chunks)
     for t, c in chunks[:ahead]:
         read_sol(t, c)
     for count, me, device in lines:

time: 11.9 us -> 11.8 us (level)
  no operation moved by 1% of the time
where the time goes in v9:
time: 11.8 us; the launch traced here: 11.7 us
  Pallas kernels  11.1 us (94%)
  between operations  0.64 us (5%)
    pallas_call x1, Pallas kernels, on_device(): pl.pallas_call(functools.partial(kernel, dims), out_shape=(pltpu.VMEM((pa...  10.4 us
    pallas_call x1, Pallas kernels, on_device(): pl.pallas_call(hand_over, out_shape=(jax.ShapeDtypeStruct(tiles.shape, f3...  0.66 us

profile of v9, /device:TPU:0, one launch (start us, length us, event | category | flops | bytes accessed | tf_op | source)
XLA Modules:
  0.0 11.7 jit_solution(1695904521098195004)
XLA Ops:
  0.6 10.4 %shard_map.59 = (f32[2,2,768]{2,1,0:T(2,128)S(1)}, f32[8,128]{1,0:T(8,128)S(1)}) custom-call(f32[2,2,3,64,512]{4,3,2,1,0:T(8,128)} %bitcast.5, f32[2,2,24,3,4,4,128]{6,5,4,3,2,1,0:T(4,128)} %bitcast.4, s32[3]{0:T(128)} %times_hbm.1, s32[3,8]{1,0:T(4,128)} %spin_hbm.1), custom_call_target="tpu_custom_call" | custom-call | tf_op jit(solution)/shard_map/pallas_call | solution.py:445
  11.0 0.7 %shard_map.60 = (f32[2,2,768]{2,1,0:T(2,128)}, f32[3,8]{1,0:T(4,128)}) custom-call(f32[2,2,768]{2,1,0:T(2,128)S(1)} %get-tuple-element.4.tiles_ref, f32[8,128]{1,0:T(8,128)S(1)} %get-tuple-element.5.norms_ref), custom_call_target="tpu_custom_call" | custom-call | tf_op jit(solution)/shard_map/pallas_call | solution.py:488

commit v10 on v9

--- a/solution.py
+++ b/solution.py
@@ -93,7 +93,7 @@
     for c in range(colors):
         for t in range(slices):
             pltpu.make_async_copy(
-                eig_hbm.at[:, t, c], eig_buf.at[c, t], eig_sem.at[min(c, 1)]
+                eig_hbm.at[:, t, c], eig_buf.at[c, t], eig_sem
             ).start()
     small_copies = [
         pltpu.make_async_copy(times_hbm, times_ref, small_sem.at[0]),
@@ -317,14 +317,10 @@
             both = partial(t, c)
             totals[t] = both if c == 0 else totals[t] + both
 
-    wait_for(eig_buf.at[0], eig_sem.at[0])
-    for t in range(slices):
-        split_eig(t, 0)
-    wait_for(eig_buf.at[pl.ds(1, colors - 1)], eig_sem.at[1])
+    wait_for(eig_buf, eig_sem)
     for c in range(colors):
-        if c:
-            for t in range(slices):
-                split_eig(t, c)
+        for t in range(slices):
+            split_eig(t, c)
         step(c)
     totals = [
         by_column(t, g[:, : parts * eigs] + g[:, parts * eigs :]) for t, g in enumerate(totals)
@@ -473,7 +469,7 @@
             pltpu.SMEM((srcs,), jnp.int32),
             pltpu.SMEM((srcs, cols), jnp.int32),
             dma((2,)),
-            dma((2,)),
+            dma,
             dma((slices * colors,)),
             dma((2,)),
             dma,

time: 11.8 us -> 11.8 us (level)
  no operation moved by 1% of the time
where the time goes in v10:
time: 11.8 us; the launch traced here: 11.7 us
  Pallas kernels  11.1 us (94%)
  between operations  0.64 us (5%)
    pallas_call x1, Pallas kernels, on_device(): pl.pallas_call(functools.partial(kernel, dims), out_shape=(pltpu.VMEM((pa...  10.4 us
    pallas_call x1, Pallas kernels, on_device(): pl.pallas_call(hand_over, out_shape=(jax.ShapeDtypeStruct(tiles.shape, f3...  0.66 us

profile of v10, /device:TPU:0, one launch (start us, length us, event | category | flops | bytes accessed | tf_op | source)
XLA Modules:
  0.0 11.7 jit_solution(16251379354062377656)
XLA Ops:
  0.6 10.4 %shard_map.59 = (f32[2,2,768]{2,1,0:T(2,128)S(1)}, f32[8,128]{1,0:T(8,128)S(1)}) custom-call(f32[2,2,3,64,512]{4,3,2,1,0:T(8,128)} %bitcast.5, f32[2,2,24,3,4,4,128]{6,5,4,3,2,1,0:T(4,128)} %bitcast.4, s32[3]{0:T(128)} %times_hbm.1, s32[3,8]{1,0:T(4,128)} %spin_hbm.1), custom_call_target="tpu_custom_call" | custom-call | tf_op jit(solution)/shard_map/pallas_call | solution.py:441
  11.0 0.7 %shard_map.60 = (f32[2,2,768]{2,1,0:T(2,128)}, f32[3,8]{1,0:T(4,128)}) custom-call(f32[2,2,768]{2,1,0:T(2,128)S(1)} %get-tuple-element.4.tiles_ref, f32[8,128]{1,0:T(8,128)S(1)} %get-tuple-element.5.norms_ref), custom_call_target="tpu_custom_call" | custom-call | tf_op jit(solution)/shard_map/pallas_call | solution.py:484
